TPU v7x, 32 devices: a whole 2x2x4 slice. The times are simulated.
32 devices in a mesh: row: 8 (over z, core), col: 4 (over y, x).
Axes of the slice: x: 2, y: 2, z: 4, core: 2. Of those that a mesh axis runs over, the one named last changes fastest.
Arguments:
- hamiltonian: bfloat16 [36864, 36864], P('row', 'col'), may hold values from -0.6 to 0.6, as said below
- start_vectors: float32 [8, 4, 9216], P(None, 'col', 'row'), may hold values from -20 to 20
Outputs:
- last_vectors: float32 [8, 36864], P(None, ('row', 'col'))
- moments: float32 [8, 4], replicated
Inputs may be any that keep to these rules, and one draw needn't show every extreme that they name: `hamiltonian`: the matrix is exactly symmetric.
All inputs are finite; a program needn't handle non-finite values.
Results may differ from a plain program's by a relative error of at most 0.0024.
Values may be sent and summed in bfloat16 or wider, within the bound.
No kernel may reach another device: no remote copies, remote signals or barrier semaphores. Data moves between devices by JAX's collectives and lax.ppermute only.
A program may use at most 128 MiB of HBM per device.

v0:
```python
import jax
import jax.numpy as jnp
from jax import lax
from jax.sharding import PartitionSpec as P

STEPS = 3
ORDER = 36864


def reduce_cols(product):
    return lax.psum_scatter(product, "col", scatter_dimension=1, tiled=True)


def reduce_rows(product):
    return lax.psum_scatter(product, "row", scatter_dimension=1, tiled=True)


def from_columns(narrow, hamiltonian):
    vec_count = narrow.shape[0]

    def accumulate(running, portion, offset):
        return lax.dot_general(
            portion, hamiltonian, (((1,), (1,)), ((), ())), preferred_element_type=jnp.float32
        )

    empty = jnp.zeros((vec_count, hamiltonian.shape[0]), jnp.float32)
    return accumulate(empty, lax.all_gather(narrow, "row", axis=1, tiled=True), jnp.int32(0))


def from_rows(narrow, hamiltonian):
    vec_count = narrow.shape[0]

    def accumulate(running, portion, offset):
        return jnp.dot(portion, hamiltonian, preferred_element_type=jnp.float32)

    empty = jnp.zeros((vec_count, hamiltonian.shape[1]), jnp.float32)
    return accumulate(empty, lax.all_gather(narrow, "col", axis=1, tiled=True), jnp.int32(0))


def reduce_each(partial_sq):
    return lax.psum(partial_sq, ("row", "col"))


def per_device(hamiltonian, start_vectors):
    current = start_vectors[:, 0, :]
    partials = [jnp.sum(current * current, axis=1) / ORDER]
    previous = current
    for level in range(STEPS):
        narrow = current.astype(jnp.bfloat16)
        if level % 2 == 0:
            applied = reduce_cols(from_columns(narrow, hamiltonian))
        else:
            applied = reduce_rows(from_rows(narrow, hamiltonian))
        if level == 0:
            following = applied
        else:
            following = 2.0 * applied - previous
        previous = current
        current = following
        partials.append(jnp.sum(current * current, axis=1) / ORDER)
    squares = jnp.stack([reduce_each(partial_sq) for partial_sq in partials], axis=1)
    moments = jnp.concatenate([squares[:, :1], 2.0 * squares[:, 1:] - squares[:, :1]], axis=1)
    return (current, moments)


def solution(mesh):
    return jax.shard_map(
        per_device,
        mesh=mesh,
        in_specs=(P("row", "col"), P(None, "col", "row")),
        out_specs=(P(None, ("row", "col")), P()),
        check_vma=False,
    )
```

profile of v0, /device:TPU:0, one launch (start us, length us, event | category | flops | bytes accessed | tf_op | source)
XLA Modules:
  0.0 266.1 jit_solution(2623065425881969994)
XLA Ops:
  7.2 0.0 reduce-scatter.4.cloned.1.call-start
  7.2 0.8 copy.12
  8.0 15.7 %all_gather.9 = bf16[8,9216]{1,0:T(8,128)(2,1)S(1)} all-gather(bf16[8,1152]{1,0:T(8,128)(2,1)S(1)} %bitcast.24), channel_id=1, replica_groups=mesh['row'=8,'col'=4] {'row'}, dimensions={1}, use_global_device_ids=true | all-gather | bytes 165888 | tf_op jit(solution)/shard_map/all_gather | solution.py:27
  23.7 0.0 copy-start.1
  23.7 31.8 %fusion.3 = f32[8,4608]{1,0:T(8,128)} fusion(bf16[8,9216]{1,0:T(8,128)(2,1)S(1)} %all_gather.9, bf16[4608,9216]{1,0:T(8,128)(2,1)} %param.2), kind=kOutput, calls=%fused_computation.16 | convolution fusion | flops 679477248 | bytes 85229568 | tf_op jit(solution)/shard_map/dot_general | solution.py:22
  55.5 0.0 reduce-scatter.4.cloned.1.call-update
  55.5 0.0 reduce-scatter.6.cloned.1.call-start
  55.6 24.7 %reduce-scatter.4.cloned.1.call-done = f32[8,1152]{1,0:T(8,128)} async-done(((f32[8,4608]{1,0:T(8,128)}), f32[8,1152]{1,0:T(8,128)}) %reduce-scatter.4.cloned.1.call-update) | async-done | bytes 36880 | tf_op jit(solution)/shard_map/reduce_scatter | solution.py:11
  80.3 0.8 convert_element_type.10
  81.0 8.2 %all_gather.10 = bf16[8,4608]{1,0:T(8,128)(2,1)S(1)} all-gather(bf16[8,1152]{1,0:T(8,128)(2,1)S(1)} %convert_element_type.10), channel_id=1, replica_groups=mesh['row'=8,'col'=4] {'col'}, dimensions={1}, use_global_device_ids=true | all-gather | bytes 92160 | tf_op jit(solution)/shard_map/all_gather | solution.py:37
  89.3 0.0 copy-start
  89.3 29.0 %fusion.4 = f32[8,9216]{1,0:T(8,128)} fusion(bf16[8,4608]{1,0:T(8,128)(2,1)S(1)} %all_gather.10, bf16[4608,9216]{1,0:T(8,128)(2,1)} %param.2), kind=kOutput, calls=%fused_computation.17 | convolution fusion | flops 679477248 | bytes 85303296 | tf_op jit(solution)/shard_map/dot_general | solution.py:34
  118.3 0.0 reduce-scatter.6.cloned.1.call-update
  118.3 0.0 reduce-scatter.8.cloned.1.call-start
  118.4 31.0 %reduce-scatter.6.cloned.1.call-done = f32[8,1152]{1,0:T(8,128)} async-done(((f32[8,9216]{1,0:T(8,128)}), f32[8,1152]{1,0:T(8,128)}) %reduce-scatter.6.cloned.1.call-update) | async-done | bytes 36880 | tf_op jit(solution)/shard_map/reduce_scatter | solution.py:15
  149.3 0.0 copy-done.1
  149.3 0.9 fusion
  150.3 14.0 %all_gather.11 = bf16[8,9216]{1,0:T(8,128)(2,1)S(1)} all-gather(bf16[8,1152]{1,0:T(8,128)(2,1)S(1)} %get-tuple-element.10), channel_id=1, replica_groups=mesh['row'=8,'col'=4] {'row'}, dimensions={1}, use_global_device_ids=true | all-gather | bytes 165888 | tf_op jit(solution)/shard_map/all_gather | solution.py:27
  164.3 31.8 %fusion.5 = f32[8,4608]{1,0:T(8,128)} fusion(bf16[8,9216]{1,0:T(8,128)(2,1)S(1)} %all_gather.11, bf16[4608,9216]{1,0:T(8,128)(2,1)} %param.2), kind=kOutput, calls=%fused_computation.18 | convolution fusion | flops 679477248 | bytes 85229568 | tf_op jit(solution)/shard_map/dot_general | solution.py:22
  196.0 0.0 reduce-scatter.8.cloned.1.call-update
  196.1 22.0 %reduce-scatter.8.cloned.1.call-done = f32[8,1152]{1,0:T(8,128)} async-done(((f32[8,4608]{1,0:T(8,128)}), f32[8,1152]{1,0:T(8,128)}) %reduce-scatter.8.cloned.1.call-update) | async-done | bytes 36880 | tf_op jit(solution)/shard_map/reduce_scatter | solution.py:11
  218.1 0.0 copy-done
  218.1 1.5 multiply_reduce_fusion
  219.6 39.3 %all-reduce = (f32[8,1]{0,1:T(1,128)S(1)}, f32[8,1]{0,1:T(1,128)S(1)}, f32[8,1]{0,1:T(1,128)S(1)}, f32[8]{0:T(128)S(1)}) all-reduce(f32[8,1]{0,1:T(1,128)S(1)} %get-tuple-element.12, f32[8,1]{0,1:T(1,128)S(1)} %multiply_bitcast_fusion.1, f32[8,1]{0,1:T(1,128)S(1)} %get-tuple-element.13, ...), channel_id=1, replica_groups=mesh['row'=8,'col'=4] {'row','col'}, use_global_device_ids=true, to_apply=%region_10.0 | all-reduce | flops 32 | bytes 256 | tf_op jit(solution)/shard_map/psum | solution.py:41
  259.0 0.6 pad_maximum_fusion
  (4 shorter events, 0.0 us)
Async XLA Ops:
  7.2 73.1 %reduce-scatter.4.cloned.1.call-start = ((), (), s32[]{:S(2)}) async-start(), calls=%async_computation.3 | async-start | bytes 184320 | tf_op jit(solution)/shard_map/reduce_scatter | solution.py:11
  23.7 125.6 %copy-start.1 = (f32[8,1,1152]{2,1,0:T(1,128)S(1)}, f32[8,1,1152]{2,1,0:T(1,128)}, u32[]{:S(2)}) copy-start(f32[8,1,1152]{2,1,0:T(1,128)} %param.3) | copy-start | bytes 110596
  55.5 93.8 %reduce-scatter.6.cloned.1.call-start = ((), (), s32[]{:S(2)}) async-start(), calls=%async_computation.4 | async-start | bytes 331776 | tf_op jit(solution)/shard_map/reduce_scatter | solution.py:15
  89.3 128.8 %copy-start = (f32[8,1152]{1,0:T(8,128)S(1)}, f32[8,1152]{1,0:T(8,128)}, u32[]{:S(2)}) copy-start(f32[8,1152]{1,0:T(8,128)} %reduce-scatter.4.cloned.1.call-done) | copy-start | bytes 110596
  118.3 99.8 %reduce-scatter.8.cloned.1.call-start = ((), (), s32[]{:S(2)}) async-start(), calls=%async_computation.5 | async-start | bytes 184320 | tf_op jit(solution)/shard_map/reduce_scatter | solution.py:11
Sparse Core Ops, SparseCore 0:
  55.6 24.5 reduce-scatter.3
  118.4 30.8 reduce-scatter.5
  196.2 21.8 reduce-scatter.7
where the time goes:
time: 267 us; the launch traced here: 266 us
  matrix products  92.5 us (35%)
  waiting for transfers between devices  77.7 us (29%)
  blocking collectives  77.3 us (29%)
  between operations  13.8 us (5%)
  other arithmetic  3.83 us (1%)
    dot_general x2, matrix products, accumulate(): lax.dot_general(portion, hamiltonian, (((1,), (1,)), ((), ())), preferred...  63.5 us
    reduce_scatter x2, waiting for transfers between devices, reduce_cols(): return lax.psum_scatter(product, 'col', scatter_dimension=1, tiled=True)  46.7 us
    psum x1, blocking collectives, reduce_each(): return lax.psum(partial_sq, ('row', 'col'))  39.3 us
    reduce_scatter x1, waiting for transfers between devices, reduce_rows(): return lax.psum_scatter(product, 'row', scatter_dimension=1, tiled=True)  31 us
    all_gather x2, blocking collectives, from_columns(): lax.all_gather(narrow, 'row', axis=1, tiled=True)  29.7 us
    dot_general x1, matrix products, accumulate(): return jnp.dot(portion, hamiltonian, preferred_element_type=jnp.float32)  29 us
    all_gather x1, blocking collectives, from_rows(): lax.all_gather(narrow, 'col', axis=1, tiled=True)  8.24 us
  transfers between devices with their start and end apart: 3, of which 3 were waited for; matrix products, arithmetic and copies ran while one was open for 0% of the time, Pallas kernels for 0%

commit v1 on v0

--- a/solution.py
+++ b/solution.py
@@ -5,6 +5,11 @@
 
 STEPS = 3
 ORDER = 36864
+
+
+def swapped_in(x, axis, dim):
+    sent = jnp.stack([x] * lax.axis_size(axis))
+    return jnp.concatenate(lax.all_to_all(sent, axis, 0, 0), axis=dim)
 
 
 def reduce_cols(product):
@@ -24,7 +29,7 @@
         )
 
     empty = jnp.zeros((vec_count, hamiltonian.shape[0]), jnp.float32)
-    return accumulate(empty, lax.all_gather(narrow, "row", axis=1, tiled=True), jnp.int32(0))
+    return accumulate(empty, swapped_in(narrow, "row", 1), jnp.int32(0))
 
 
 def from_rows(narrow, hamiltonian):

time: 267 us -> 259 us (0.970)
  blocking collectives: 77.3 us -> 70.1 us
    all_gather x2 -> x0, blocking collectives: 29.7 us -> none  [from_columns(): lax.all_gather(narrow, 'row', axis=1, tiled=True)]
    all_to_all x0 -> x2, blocking collectives: none -> 22.5 us  [swapped_in(): return jnp.concatenate(lax.all_to_all(sent, axis, 0, 0), axis=dim)]
where the time goes in v1:
time: 259 us; the launch traced here: 258 us
  matrix products  92.5 us (36%)
  waiting for transfers between devices  77 us (30%)
  blocking collectives  70.1 us (27%)
  between operations  13.8 us (5%)
  other arithmetic  3.83 us (1%)
    dot_general x2, matrix products, accumulate(): lax.dot_general(portion, hamiltonian, (((1,), (1,)), ((), ())), preferred...  63.5 us
    reduce_scatter x2, waiting for transfers between devices, reduce_cols(): return lax.psum_scatter(product, 'col', scatter_dimension=1, tiled=True)  46 us
    psum x1, blocking collectives, reduce_each(): return lax.psum(partial_sq, ('row', 'col'))  39.3 us
    reduce_scatter x1, waiting for transfers between devices, reduce_rows(): return lax.psum_scatter(product, 'row', scatter_dimension=1, tiled=True)  30.9 us
    dot_general x1, matrix products, accumulate(): return jnp.dot(portion, hamiltonian, preferred_element_type=jnp.float32)  29 us
    all_to_all x2, blocking collectives, swapped_in(): return jnp.concatenate(lax.all_to_all(sent, axis, 0, 0), axis=dim)  22.5 us
    all_gather x1, blocking collectives, from_rows(): lax.all_gather(narrow, 'col', axis=1, tiled=True)  8.26 us
  transfers between devices with their start and end apart: 3, of which 3 were waited for; matrix products, arithmetic and copies ran while one was open for 0% of the time, Pallas kernels for 0%

profile of v1, /device:TPU:0, one launch (start us, length us, event | category | flops | bytes accessed | tf_op | source)
XLA Modules:
  0.0 258.1 jit_solution(14730327101020975513)
XLA Ops:
  7.2 0.0 reduce-scatter.4.cloned.1.call-start
  7.2 0.8 copy.12
  8.0 13.1 %all_to_all.10 = bf16[8,8,1152]{2,1,0:T(8,128)(2,1)S(1)} all-to-all(bf16[8,8,1152]{2,1,0:T(8,128)(2,1)S(1)} %stack.14), channel_id=1, replica_groups=mesh['row'=8,'col'=4] {'row'}, dimensions={0} | all-to-all | bytes 294912 | tf_op jit(solution)/shard_map/all_to_all | solution.py:12
  21.1 0.0 copy-start.1
  21.1 31.8 %fusion.3 = f32[8,4608]{1,0:T(8,128)} fusion(bf16[8,9216]{1,0:T(8,128)(2,1)S(1)} %bitcast.30, bf16[4608,9216]{1,0:T(8,128)(2,1)} %param.2), kind=kOutput, calls=%fused_computation.16 | convolution fusion | flops 679477248 | bytes 85229568 | tf_op jit(solution)/shard_map/dot_general | solution.py:27
  52.9 0.0 reduce-scatter.4.cloned.1.call-update
  52.9 0.0 reduce-scatter.6.cloned.1.call-start
  53.0 22.9 %reduce-scatter.4.cloned.1.call-done = f32[8,1152]{1,0:T(8,128)} async-done(((f32[8,4608]{1,0:T(8,128)}), f32[8,1152]{1,0:T(8,128)}) %reduce-scatter.4.cloned.1.call-update) | async-done | bytes 36880 | tf_op jit(solution)/shard_map/reduce_scatter | solution.py:16
  75.9 0.8 convert_element_type.12
  76.7 8.3 %all_gather.3 = bf16[8,4608]{1,0:T(8,128)(2,1)S(1)} all-gather(bf16[8,1152]{1,0:T(8,128)(2,1)S(1)} %convert_element_type.12), channel_id=1, replica_groups=mesh['row'=8,'col'=4] {'col'}, dimensions={1}, use_global_device_ids=true | all-gather | bytes 92160 | tf_op jit(solution)/shard_map/all_gather | solution.py:42
  84.9 0.0 copy-start
  84.9 29.0 %fusion.4 = f32[8,9216]{1,0:T(8,128)} fusion(bf16[8,4608]{1,0:T(8,128)(2,1)S(1)} %all_gather.3, bf16[4608,9216]{1,0:T(8,128)(2,1)} %param.2), kind=kOutput, calls=%fused_computation.17 | convolution fusion | flops 679477248 | bytes 85303296 | tf_op jit(solution)/shard_map/dot_general | solution.py:39
  113.9 0.0 reduce-scatter.6.cloned.1.call-update
  114.0 0.0 reduce-scatter.8.cloned.1.call-start
  114.0 30.9 %reduce-scatter.6.cloned.1.call-done = f32[8,1152]{1,0:T(8,128)} async-done(((f32[8,9216]{1,0:T(8,128)}), f32[8,1152]{1,0:T(8,128)}) %reduce-scatter.6.cloned.1.call-update) | async-done | bytes 36880 | tf_op jit(solution)/shard_map/reduce_scatter | solution.py:20
  144.9 0.0 copy-done.1
  144.9 0.9 fusion
  145.9 9.4 %all_to_all.11 = bf16[8,8,1152]{2,1,0:T(8,128)(2,1)S(1)} all-to-all(bf16[8,8,1152]{2,1,0:T(8,128)(2,1)S(1)} %stack.15), channel_id=1, replica_groups=mesh['row'=8,'col'=4] {'row'}, dimensions={0} | all-to-all | bytes 294912 | tf_op jit(solution)/shard_map/all_to_all | solution.py:12
  155.2 31.8 %fusion.5 = f32[8,4608]{1,0:T(8,128)} fusion(bf16[8,9216]{1,0:T(8,128)(2,1)S(1)} %bitcast.31, bf16[4608,9216]{1,0:T(8,128)(2,1)} %param.2), kind=kOutput, calls=%fused_computation.18 | convolution fusion | flops 679477248 | bytes 85229568 | tf_op jit(solution)/shard_map/dot_general | solution.py:27
  187.0 0.0 reduce-scatter.8.cloned.1.call-update
  187.1 23.1 %reduce-scatter.8.cloned.1.call-done = f32[8,1152]{1,0:T(8,128)} async-done(((f32[8,4608]{1,0:T(8,128)}), f32[8,1152]{1,0:T(8,128)}) %reduce-scatter.8.cloned.1.call-update) | async-done | bytes 36880 | tf_op jit(solution)/shard_map/reduce_scatter | solution.py:16
  210.1 0.0 copy-done
  210.1 1.5 multiply_reduce_fusion
  211.7 39.3 %all-reduce = (f32[8,1]{0,1:T(1,128)S(1)}, f32[8,1]{0,1:T(1,128)S(1)}, f32[8,1]{0,1:T(1,128)S(1)}, f32[8]{0:T(128)S(1)}) all-reduce(f32[8,1]{0,1:T(1,128)S(1)} %get-tuple-element.12, f32[8,1]{0,1:T(1,128)S(1)} %multiply_bitcast_fusion.1, f32[8,1]{0,1:T(1,128)S(1)} %get-tuple-element.13, ...), channel_id=1, replica_groups=mesh['row'=8,'col'=4] {'row','col'}, use_global_device_ids=true, to_apply=%region_10.0 | all-reduce | flops 32 | bytes 256 | tf_op jit(solution)/shard_map/psum | solution.py:46
  251.0 0.6 pad_maximum_fusion
  (6 shorter events, 0.1 us)
Async XLA Ops:
  7.2 68.7 %reduce-scatter.4.cloned.1.call-start = ((), (), s32[]{:S(2)}) async-start(), calls=%async_computation.5 | async-start | bytes 184320 | tf_op jit(solution)/shard_map/reduce_scatter | solution.py:16
  21.1 123.8 %copy-start.1 = (f32[8,1,1152]{2,1,0:T(1,128)S(1)}, f32[8,1,1152]{2,1,0:T(1,128)}, u32[]{:S(2)}) copy-start(f32[8,1,1152]{2,1,0:T(1,128)} %param.3) | copy-start | bytes 110596
  52.9 92.0 %reduce-scatter.6.cloned.1.call-start = ((), (), s32[]{:S(2)}) async-start(), calls=%async_computation.6 | async-start | bytes 331776 | tf_op jit(solution)/shard_map/reduce_scatter | solution.py:20
  84.9 125.2 %copy-start = (f32[8,1152]{1,0:T(8,128)S(1)}, f32[8,1152]{1,0:T(8,128)}, u32[]{:S(2)}) copy-start(f32[8,1152]{1,0:T(8,128)} %reduce-scatter.4.cloned.1.call-done) | copy-start | bytes 110596
  114.0 96.2 %reduce-scatter.8.cloned.1.call-start = ((), (), s32[]{:S(2)}) async-start(), calls=%async_computation.7 | async-start | bytes 184320 | tf_op jit(solution)/shard_map/reduce_scatter | solution.py:16
Sparse Core Ops, SparseCore 0:
  53.0 22.8 reduce-scatter.3
  114.1 30.8 reduce-scatter.5
  187.2 22.9 reduce-scatter.7
